TPU v7x, 128 devices: a whole 4x4x4 slice. The times are simulated.
128 devices in a mesh: tm: 8 (over y, core), lat: 16 (over x, z).
Axes of the slice: x: 4, y: 4, z: 4, core: 2. Of those that a mesh axis runs over, the one named last changes fastest.
Arguments:
- trajectory: float32 [8, 64, 64, 2048], P('tm', 'lat'), may hold values from -6 to 6
- diffusivity: float32 [8, 64, 64, 2048], P('tm', 'lat'), may hold values from 0.02 to 0.24
- adjoint_end: bfloat16 [64, 64, 2048], P('lat'), may hold values from -6 to 6
- obs_jac: bfloat16 [12288, 128, 128], P(('tm', 'lat')), may hold values from -0.5 to 0.5
- obs_value: float32 [12288, 128], P(('tm', 'lat')), may hold values from -6 to 6
- obs_weight: float32 [12288, 128], P(('tm', 'lat')), may hold values from 0.3 to 3
- obs_valid: int32 [12288, 128], P(('tm', 'lat')), may hold values 0 or 1
- obs_owner: int32 [12288, 1], P(('tm', 'lat')), may hold values from 0 to 127; in each aligned block of 96 rows (0 to 95, 96 to 191, ...) at most 2 rows name the same one
- obs_tile: int32 [12288], P(('tm', 'lat')), may hold values from 0 to 4095
Outputs:
- adjoint: float32 [8, 64, 64, 2048], P('tm', 'lat')
Inputs may be any that keep to these rules, and one draw needn't show every extreme that they name: `obs_owner`: among the 96 blocks of one device, no owner is named more than 2 times, a bound that some block reaches.
All inputs are finite; a program needn't handle non-finite values. No bound on the sum of `obs_valid` on one device may be relied on, other than what follows from the above.
Results may differ from a plain program's by a relative error of at most 0.0024.
Values may be sent and summed in bfloat16 or wider, within the bound.
A program may use at most 128 MiB of HBM per device.

v0:
```python
import jax
import jax.numpy as jnp
from jax import lax
from jax.experimental import pallas as pl
from jax.experimental.pallas import tpu as pltpu
from jax.sharding import PartitionSpec as P

f32, bf16, i16, i32 = jnp.float32, jnp.bfloat16, jnp.int16, jnp.int32
MESH = pl.DeviceIdType.MESH

DEV = 128
NB = 96
BANDS = 12
CHUNK = 64
KMID, KSCALE = 0.13, 0.11 / 32700.0


def split(x):
    hi = x.astype(bf16)
    return hi, (x - hi.astype(f32)).astype(bf16)


def dot(a, b, ca, cb):
    return lax.dot_general(a, b, (((ca,), (cb,)), ((), ())), preferred_element_type=f32)


def iota(shape, dim):
    return lax.broadcasted_iota(i32, shape, dim)


def kernel(
    traj_ref, kap_ref, end_ref, jac_ref, val_ref, wgt_ref, vld_ref, own_ref, til_ref,
    out_ref,
    TRJ, KIN, EIN, JAC, E32,
    AS, AR, TT, LOH, ACC, BS, BR, S3, PR, CS, CR, RT,
    KS, KR, ES, EN, W, WT, OS, OR,
    lsem, asem, bsem, csem, ksend, krecv, esem, osem,
):
    tm = lax.axis_index("tm")
    lat = lax.axis_index("lat")
    me = tm * 16 + lat
    half = lax.rem(tm, 2)
    pair = lax.div(tm, 2)
    level = pair * 16 + lat
    lb_me = lat - 4 * half
    in_me = (lb_me >= 0) & (lb_me < BANDS)

    loads = [
        pltpu.make_async_copy(traj_ref, TRJ, lsem.at[0]),
        pltpu.make_async_copy(jac_ref, JAC, lsem.at[1]),
        pltpu.make_async_copy(
            end_ref.at[:, pl.ds(pl.multiple_of(pair * 16, 16), 16), :], EIN, lsem.at[2]
        ),
    ]
    for h in range(16):
        loads.append(
            pltpu.make_async_copy(
                kap_ref.at[:, :, pl.ds(h * 128, 128)], KIN.at[h], lsem.at[3 + h]
            )
        )
    for copy in loads:
        copy.start()

    own = own_ref[...]
    eye = iota((NB, NB), 0) == iota((NB, NB), 1)
    own_row = jnp.sum(jnp.where(eye, own.astype(f32), 0.0), axis=0, keepdims=True)
    til = jnp.sum(jnp.where(eye, til_ref[...].astype(f32), 0.0), axis=1, keepdims=True)
    same = (own.astype(f32) == own_row) & (iota((NB, NB), 1) < iota((NB, NB), 0))
    rank = jnp.sum(jnp.where(same, 1.0, 0.0), axis=1, keepdims=True).astype(i32)
    place = rank * DEV + own
    hit = iota((NB, 2 * DEV), 1) == place
    M = jnp.where(hit, 1.0, 0.0).astype(bf16)
    ids = jnp.sum(jnp.where(hit, til + 1.0, 0.0), axis=0, keepdims=True)
    AS[0, 0:1, :] = ids[:, :DEV]
    AS[0, 1:2, :] = ids[:, DEV:]
    AR[me] = AS[0]

    def peers(fn):
        def step(i, carry):
            d = lax.rem(me + i, DEV)
            fn(d, lax.div(d, 16), lax.rem(d, 16))
            return carry

        lax.fori_loop(1, DEV, step, 0)

    def send_a(d, t, l):
        pltpu.make_async_remote_copy(
            AS.at[0], AR.at[me], asem.at[0], asem.at[1], device_id=(t, l), device_id_type=MESH
        ).start()

    peers(send_a)

    loads[2].wait()
    for h in range(16):
        E32[h] = EIN[:, :, h * 128 : (h + 1) * 128].astype(f32)
    e2 = E32.reshape(16 * 4 * 16, 128)

    def end_level(l, carry):
        for r in range(4):
            ES[l, r * 16 : (r + 1) * 16, :] = e2[pl.ds(r * 16 + l, 16, stride=64), :].astype(bf16)
        return carry

    lax.fori_loop(0, 16, end_level, 0)

    @pl.when(in_me)
    def _():
        EN[lb_me] = ES[lat]

        def send_e(i, carry):
            l = lax.rem(lat + i, 16)
            pltpu.make_async_remote_copy(
                ES.at[l], EN.at[lb_me], esem.at[0], esem.at[1], device_id=(tm, l), device_id_type=MESH
            ).start()
            return carry

        lax.fori_loop(1, 16, send_e, 0)

    for copy in loads[3:]:
        copy.wait()
    k2 = KIN.reshape(16 * 4 * 64, 128)

    def kap_level(l, carry):
        for r in range(4):
            k = k2[pl.ds(r * 64 + l, 16, stride=256), :]
            q = jnp.round((k - KMID) * (1.0 / KSCALE))
            KS[l, r * 16 : (r + 1) * 16, :] = q.astype(i32).astype(i16)
        return carry

    lax.fori_loop(0, 64, kap_level, 0)

    def send_k(d, t, l):
        c = lax.rem(t, 2)
        lb = lat - 4 * c

        @pl.when((lb >= 0) & (lb < BANDS))
        def _():
            pltpu.make_async_remote_copy(
                KS.at[lax.div(t, 2) * 16 + l], KR.at[tm * BANDS + lb], ksend.at[c], krecv,
                device_id=(t, l), device_id_type=MESH,
            ).start()

    peers(send_k)

    @pl.when(in_me)
    def _():
        KR[tm * BANDS + lb_me] = KS[level]

    def wait_n(buf, n, sem):
        part = buf.at[pl.ds(0, n)]
        pltpu.make_async_copy(part, part, sem).wait()

    wait_n(AR, DEV - 1, asem.at[1])
    for s in range(2):
        TT[s] = AR[:, s, :].T
    tid = jnp.concatenate([TT[s, pl.ds(me, 1), :] for s in range(2)], axis=1).astype(i32) - 1
    low = (tid & 127) * 2
    group = jnp.concatenate([tid >> 7, tid >> 7], axis=1)
    LOH[...] = jnp.where(
        iota((256, 512), 0) == jnp.concatenate([low, low + 1], axis=1), 1.0, 0.0
    ).astype(bf16)
    ACC[...] = jnp.zeros((64, 512), f32)
    loads[0].wait()

    def gather_row(r, carry):
        total = ACC[...]
        for g in range(8):
            hi, lo = split(TRJ[r, :, g * 256 : (g + 1) * 256])
            y = dot(jnp.concatenate([hi, lo], axis=0), LOH[...], 1, 0)
            total = total + jnp.where(group == r * 8 + g, y[:64] + y[64:], 0.0)
        ACC[...] = total
        return carry

    lax.fori_loop(0, 4, gather_row, 0)
    for s in range(2):
        x = jnp.concatenate(
            [ACC[:, s * 128 : (s + 1) * 128], ACC[:, 256 + s * 128 : 256 + (s + 1) * 128]], axis=0
        )
        BS[:, s, :] = x.T
    BR[me] = BS[me]

    def send_b(d, t, l):
        pltpu.make_async_remote_copy(
            BS.at[d], BR.at[me], bsem.at[0], bsem.at[1], device_id=(t, l), device_id_type=MESH
        ).start()

    peers(send_b)

    S3[...] = jnp.zeros((NB, 8, 128), f32)
    swap = jnp.where(
        iota((128, 128), 1) == (iota((128, 128), 0) & 63) * 2 + (iota((128, 128), 0) >> 6), 1.0, 0.0
    ).astype(bf16)
    wait_n(BR, DEV - 1, bsem.at[1])
    parts = [split(BR[:, s, :]) for s in range(2)]
    for p in range(2):
        mine = dot(M[:, :DEV], parts[0][p], 1, 0) + dot(M[:, DEV:], parts[1][p], 1, 0)
        S3[:, p, :] = dot(mine.astype(bf16), swap, 1, 0)
    loads[1].wait()

    def predict(b, carry):
        PR[b] = dot(S3[b].astype(bf16), JAC[b], 1, 1)
        return carry

    lax.fori_loop(0, NB, predict, 0, unroll=8)
    weight = wgt_ref[...] * vld_ref[...].astype(f32)
    resid = weight * (val_ref[...] - (PR[:, 0, :] + PR[:, 1, :]))
    for p, part in enumerate(split(resid)):
        S3[:, p, :] = part.astype(f32)

    def adjoin(b, carry):
        PR[b] = dot(S3[b].astype(bf16), JAC[b], 1, 0)
        return carry

    lax.fori_loop(0, NB, adjoin, 0, unroll=8)
    placed = jnp.zeros((128, 256), f32)
    for part in split(PR[:, 0, :] + PR[:, 1, :]):
        placed = placed + dot(dot(part, swap, 1, 1).astype(bf16), M, 0, 0)
    for s in range(2):
        for w in range(2):
            CS[:, s * 2 + w, :] = placed[w * 64 : (w + 1) * 64, s * 128 : (s + 1) * 128]
    CR[me] = CS[level]

    def send_c(d, t, l):
        pltpu.make_async_remote_copy(
            CS.at[lax.div(t, 2) * 16 + l], CR.at[me], csem.at[0], csem.at[1],
            device_id=(t, l), device_id_type=MESH,
        ).start()

    peers(send_c)

    @pl.when(in_me)
    def _():
        wait_n(EN, BANDS - 1, esem.at[1])
        wait_n(KR, 8 * BANDS - 1, krecv)

    @pl.when(jnp.logical_not(in_me))
    def _():
        wait_n(EN, BANDS, esem.at[1])
        wait_n(KR, 8 * BANDS, krecv)

    for lb in range(BANDS):
        W[lb * 4 : lb * 4 + 4] = EN[lb].astype(f32).reshape(4, 16, 128)
    WT[0] = jnp.zeros((16, 128), f32)
    WT[49] = jnp.zeros((16, 128), f32)
    lane = iota((8, 16, 128), 2)

    def substeps(s):
        def one(_, carry):
            for g in range(6):
                k = KR[pl.ds(s * BANDS + g * 2, 2)].astype(i32).astype(f32) * KSCALE + KMID
                WT[1 + g * 8 : 9 + g * 8] = k.reshape(8, 16, 128) * W[g * 8 : g * 8 + 8]
            for g in range(6):
                x = WT[1 + g * 8 : 9 + g * 8]
                a = pltpu.roll(x, 1, axis=2)
                b = pltpu.roll(x, 127, axis=2)
                a = jnp.where(lane == 0, pltpu.roll(a, 1, axis=1), a)
                b = jnp.where(lane == 127, pltpu.roll(b, 15, axis=1), b)
                sides = (WT[2 + g * 8 : 10 + g * 8] + WT[g * 8 : g * 8 + 8]) + (a + b)
                W[g * 8 : g * 8 + 8] = W[g * 8 : g * 8 + 8] + (sides - 4.0 * x)
            return carry

        lax.fori_loop(0, 2, one, 0)

    def finish(s):
        def band(lb, carry):
            o = s * 16 + lb + 4 * half
            tid = jnp.concatenate([TT[k, pl.ds(o, 1), :] for k in range(2)], axis=1).astype(i32) - 1
            low = (tid & 63) * 2
            right = jnp.where(
                iota((128, 512), 0) == jnp.concatenate([low, low + 1], axis=1), 1.0, 0.0
            ).astype(bf16)
            mask = iota((64, 256), 0) == (tid >> 6)
            left = []
            for w in range(2):
                term = jnp.concatenate([RT[k * 2 + w, pl.ds(o, 1), :] for k in range(2)], axis=1)
                left.append([jnp.where(mask, p.astype(f32), 0.0).astype(bf16) for p in split(term)])
            lhs = jnp.concatenate(
                [jnp.concatenate([left[0][p], left[1][p]], axis=1) for p in range(2)], axis=0
            )
            y = dot(lhs, right, 1, 1)
            rows = pl.ds(lb * 4, 4)
            W[rows] = W[rows] + (y[:64] + y[64:]).reshape(4, 16, 128)
            return carry

        lax.fori_loop(0, BANDS, band, 0)

        def deliver(j, carry):
            OS[s * 8 + j] = W[pl.ds(half * 16 + j * 4, 4)].reshape(CHUNK, 128).astype(bf16)
            to = half * 8 + j

            @pl.when((s == tm) & (to == lat))
            def _():
                OR[level] = OS[s * 8 + j]

            @pl.when((s != tm) | (to != lat))
            def _():
                pltpu.make_async_remote_copy(
                    OS.at[s * 8 + j], OR.at[level], osem.at[0], osem.at[1],
                    device_id=(s, to), device_id_type=MESH,
                ).start()

            return carry

        lax.fori_loop(0, 8, deliver, 0)

    substeps(7)
    wait_n(CR, DEV - 1, csem.at[1])
    for q in range(4):
        RT[q] = CR[:, q, :].T

    def section(i, carry):
        s = 7 - i
        finish(s)
        W[...] = W[...].astype(bf16).astype(f32)
        substeps(s - 1)
        return carry

    lax.fori_loop(0, 7, section, 0)
    finish(0)

    mine_o = lax.div(lat, 8) == half

    @pl.when(mine_o)
    def _():
        wait_n(OR, 63, osem.at[1])

    @pl.when(jnp.logical_not(mine_o))
    def _():
        wait_n(OR, 64, osem.at[1])

    def store(l, carry):
        for r in range(4):
            out_ref[pl.ds(r * 64 + l, 16, stride=256), :] = OR[l, r * 16 : (r + 1) * 16, :].astype(f32)
        return carry

    lax.fori_loop(0, 64, store, 0)

    wait_n(AR, DEV - 1, asem.at[0])
    wait_n(BS, DEV - 1, bsem.at[0])
    wait_n(CR, DEV - 1, csem.at[0])

    @pl.when(in_me)
    def _():
        wait_n(ES, 15, esem.at[0])

    for c in range(2):
        inside = (lat < BANDS) if c == 0 else (lat >= 4)

        @pl.when(inside & (half == c))
        def _():
            wait_n(KS, 63, ksend.at[c])

        @pl.when(inside & (half != c))
        def _():
            wait_n(KS, 64, ksend.at[c])

    @pl.when(mine_o)
    def _():
        wait_n(OS, 63, osem.at[0])

    @pl.when(jnp.logical_not(mine_o))
    def _():
        wait_n(OS, 64, osem.at[0])


def per_device(traj, kap, end, jac, val, wgt, vld, own, til):
    hbm = pl.BlockSpec(memory_space=pl.ANY)
    vmem = pl.BlockSpec(memory_space=pltpu.VMEM)
    dma = pltpu.SemaphoreType.DMA
    V = pltpu.VMEM
    out = pl.pallas_call(
        kernel,
        out_shape=jax.ShapeDtypeStruct((16 * 4 * 64, 128), f32),
        in_specs=[hbm] * 4 + [vmem] * 5,
        out_specs=vmem,
        scratch_shapes=[
            V((4, 64, 2048), f32), V((16, 4, 64, 128), f32), V((4, 16, 2048), bf16),
            V((NB, 128, 128), bf16), V((16, 4, 16, 128), f32),
            V((1, 2, 128), f32), V((DEV, 2, 128), f32), V((2, 128, 128), f32),
            V((256, 512), bf16), V((64, 512), f32), V((DEV, 2, 128), f32), V((DEV, 2, 128), f32),
            V((NB, 8, 128), f32), V((NB, 8, 128), f32), V((64, 4, 128), f32), V((DEV, 4, 128), f32),
            V((4, 128, 128), f32),
            V((64, CHUNK, 128), i16), V((8 * BANDS, CHUNK, 128), i16),
            V((16, CHUNK, 128), bf16), V((BANDS, CHUNK, 128), bf16),
            V((48, 16, 128), f32), V((50, 16, 128), f32),
            V((64, CHUNK, 128), bf16), V((64, CHUNK, 128), bf16),
            dma((19,)), dma((2,)), dma((2,)), dma((2,)), dma((2,)), dma, dma((2,)), dma((2,)),
        ],
        compiler_params=pltpu.CompilerParams(has_side_effects=True, vmem_limit_bytes=56 << 20),
        name="adjoint_sweep",
    )(traj[0], kap[0], end, jac, val, wgt, vld, own, til.reshape(1, NB))
    return out.reshape(16, 4, 64, 128).transpose(1, 2, 0, 3).reshape(1, 4, 64, 2048)


def solution(mesh):
    both = ("tm", "lat")
    in_specs = (
        P("tm", "lat", None, None),
        P("tm", "lat", None, None),
        P("lat", None, None),
        P(both, None, None),
        P(both, None),
        P(both, None),
        P(both, None),
        P(both, None),
        P(both),
    )
    return jax.shard_map(
        per_device, mesh=mesh, in_specs=in_specs, out_specs=P("tm", "lat", None, None),
        check_vma=False,
    )
```

profile of v0, /device:TPU:1, one launch (start us, length us, event | category | flops | bytes accessed | tf_op | source)
XLA Modules:
  0.0 109.8 jit_solution(12513426550970687585)
XLA Ops:
  0.0 1.4 %copy.10.own_ref = s32[96,1]{1,0:T(8,128)} copy(s32[96,1]{0,1:T(1,128)} %param.16) | data formatting | bytes 768 | tf_op args[7]
  1.4 104.2 %adjoint_sweep.1 = f32[4096,128]{1,0:T(8,128)} custom-call(f32[4,64,2048]{2,1,0:T(8,128)} %bitcast.9, f32[4,64,2048]{2,1,0:T(8,128)} %bitcast.10, bf16[4,64,2048]{2,1,0:T(8,128)(2,1)} %end_ref.1, bf16[96,128,128]{2,1,0:T(8,128)(2,1)} %jac_ref.1, f32[96,128]{1,0:T(8,128)} %val_ref.1, f32[96,128]{1,0:T(8,128)} %wgt_ref.1, s32[96,128]{1,0:T(8,128)} %vld_ref.1, ...), custom_call_target="tpu_custom_call" | custom-call | tf_op jit(solution)/shard_map/adjoint_sweep/pallas_call | solution.py:370
  105.5 2.8 %copy.11 = f32[4,64,16,128]{3,2,1,0:T(8,128)S(1)} copy(f32[4,64,16,128]{3,1,0,2:T(8,128)} %bitcast.8) | data formatting | bytes 4194304 | tf_op jit(solution)/shard_map/transpose | solution.py:391
  108.3 1.5 %reshape.11 = f32[1,4,64,2048]{3,2,1,0:T(8,128)} reshape(f32[4,64,16,128]{3,2,1,0:T(8,128)S(1)} %copy.11) | data formatting | bytes 4194304 | tf_op jit(solution)/shard_map/reshape | solution.py:391
where the time goes:
time: 110 us
  Pallas kernels  104 us (95%)
  local copies, waits for them, and re-layouts  5.67 us (5%)
    pallas_call x1, Pallas kernels, per_device(): pl.pallas_call(kernel, out_shape=jax.ShapeDtypeStruct((16 * 4 * 64, 128),...  104 us
    transpose x1, local copies, waits for them, and re-layouts, per_device(): out.reshape(16, 4, 64, 128).transpose(1, 2, 0, 3).reshape(1, 4, 64, 2048)  2.81 us

commit v1 on v0

v1 whole, which is shorter than its diff:
```python
import jax
import jax.numpy as jnp
from jax import lax
from jax.experimental import pallas as pl
from jax.experimental.pallas import tpu as pltpu
from jax.sharding import PartitionSpec as P

f32, bf16, i16, i32 = jnp.float32, jnp.bfloat16, jnp.int16, jnp.int32
MESH = pl.DeviceIdType.MESH

DEV = 128
NB = 96
BANDS = 12
KFIRST = 32
CHUNK = 64
KMID, KSCALE = 0.13, 0.11 / 32700.0


def split(x):
    hi = x.astype(bf16)
    return hi, (x - hi.astype(f32)).astype(bf16)


def dot(a, b, ca, cb):
    return lax.dot_general(a, b, (((ca,), (cb,)), ((), ())), preferred_element_type=f32)


def iota(shape, dim):
    return lax.broadcasted_iota(i32, shape, dim)


def kernel(
    traj_ref, kap_ref, end_ref, jac_ref, val_ref, wgt_ref, vld_ref, own_ref, til_ref,
    out_ref,
    TRJ, KIN, KQ, EIN, EQ, JAC,
    AS, AR, TT, LOH, ACC, BS, BR, S3, PR, CS, CR, RT, OHR,
    KS, KR, ES, EN, W, WT, KF, OS, OR,
    lsem, asem, bsem, csem, ksem, esem, fsem, osem,
):
    tm = lax.axis_index("tm")
    lat = lax.axis_index("lat")
    me = tm * 16 + lat
    half = lax.rem(tm, 2)
    pair = lax.div(tm, 2)
    level = pair * 16 + lat
    mate = tm + 1 - 2 * half
    side = lax.div(lat, 8)
    home = side == half
    away = side != half

    def peers(fn):
        def step(i, carry):
            d = lax.rem(me + i, DEV)
            fn(d, lax.div(d, 16), lax.rem(d, 16))
            return carry

        lax.fori_loop(1, DEV, step, 0)

    def send(src, dst, sems, t, l):
        return pltpu.make_async_remote_copy(
            src, dst, sems.at[0], sems.at[1], device_id=(t, l), device_id_type=MESH
        )

    def wait_n(buf, n, sem):
        part = buf.at[pl.ds(0, n)]
        pltpu.make_async_copy(part, part, sem).wait()

    def wait_home(buf, n, sem):
        @pl.when(home)
        def _():
            wait_n(buf, n - 1, sem)

        @pl.when(away)
        def _():
            wait_n(buf, n, sem)

    loads = [
        pltpu.make_async_copy(kap_ref, KIN, lsem.at[0]),
        pltpu.make_async_copy(
            end_ref.at[:, pl.ds(pl.multiple_of(pair * 16, 16), 16), :], EIN, lsem.at[1]
        ),
        pltpu.make_async_copy(traj_ref, TRJ, lsem.at[2]),
        pltpu.make_async_copy(jac_ref, JAC, lsem.at[3]),
    ]
    for copy in loads:
        copy.start()
    barrier = pltpu.get_barrier_semaphore()
    peers(
        lambda d, t, l: pl.semaphore_signal(barrier, 1, device_id=(t, l), device_id_type=MESH)
    )

    eye = iota((NB, NB), 0) == iota((NB, NB), 1)
    own_row = own_ref[...].astype(f32)
    own = jnp.sum(jnp.where(eye, own_row, 0.0), axis=1, keepdims=True)
    til = jnp.sum(jnp.where(eye, til_ref[...].astype(f32), 0.0), axis=1, keepdims=True)
    same = (own == own_row) & (iota((NB, NB), 1) < iota((NB, NB), 0))
    rank = jnp.sum(jnp.where(same, 1.0, 0.0), axis=1, keepdims=True)
    hit = iota((NB, 2 * DEV), 1) == (rank * DEV + own).astype(i32)
    M = jnp.where(hit, 1.0, 0.0).astype(bf16)
    ids = jnp.sum(jnp.where(hit, til + 1.0, 0.0), axis=0, keepdims=True)
    AS[0, 0:1, :] = ids[:, :DEV]
    AS[0, 1:2, :] = ids[:, DEV:]
    AR[me] = AS[0]

    apart = jnp.where(
        iota((256, 256), 0) == (iota((256, 256), 1) & 127) * 2 + (iota((256, 256), 1) >> 7), 1.0, 0.0
    ).astype(bf16)

    loads[0].wait()

    def kap_row(r, carry):
        for g in range(8):
            q = jnp.round((KIN[r, :, g * 256 : (g + 1) * 256] - KMID) * (1.0 / KSCALE))
            a = jnp.round(q * (1.0 / 256.0))
            b = q - a * 256.0
            y = dot(jnp.concatenate([a, b], axis=0).astype(bf16), apart, 1, 0)
            y = y[:64] * 256.0 + y[64:]
            rows = pl.ds(pl.multiple_of(r * 64, 64), 64)
            KQ[g, rows, :] = y[:, :128]
            KQ[8 + g, rows, :] = y[:, 128:]
        return carry

    lax.fori_loop(0, 4, kap_row, 0)
    k2 = KQ.reshape(16 * 256, 128)

    def kap_level(l, carry):
        for r in range(4):
            q = k2[pl.ds(r * 64 + l, 16, stride=256), :]
            KS[l, r * 16 : (r + 1) * 16, :] = q.astype(i32).astype(i16)
        return carry

    lax.fori_loop(0, 64, kap_level, 0, unroll=2)

    loads[1].wait()
    for r in range(4):
        for g in range(8):
            y = dot(EIN[r, :, g * 256 : (g + 1) * 256], apart, 1, 0)
            EQ[g, r * 16 : (r + 1) * 16, :] = y[:, :128]
            EQ[8 + g, r * 16 : (r + 1) * 16, :] = y[:, 128:]
    e2 = EQ.reshape(16 * 64, 128)

    def end_level(l, carry):
        for r in range(4):
            rows = e2[pl.ds(r * 16 + half * 8 + l, 16, stride=64), :]
            ES[l, r * 16 : (r + 1) * 16, :] = rows.astype(bf16)
        return carry

    lax.fori_loop(0, 8, end_level, 0)
    lb_me = lat - 4 * side

    @pl.when(home)
    def _():
        KR[lb_me * 8 + tm] = KS[level]
        EN[lb_me] = ES[lat - 8 * half]

    pl.semaphore_wait(barrier, DEV - 1)
    peers(lambda d, t, l: send(AS.at[0], AR.at[me], asem, t, l).start())

    def send_k(lo, hi):
        def step(i, carry):
            l = lax.rem(level + i * 27, 64)

            @pl.when((i > 0) | away)
            def _():
                send(
                    KS.at[l], KR.at[lb_me * 8 + tm], ksem, lax.div(l, 16) * 2 + side, lax.rem(l, 16)
                ).start()

            return carry

        lax.fori_loop(lo, hi, step, 0)

    def send_e(i, carry):
        l = half * 8 + i

        @pl.when((l != lat) | away)
        def _():
            send(ES.at[i], EN.at[lb_me], esem, pair * 2 + side, l).start()

        return carry

    send_k(0, KFIRST)

    wait_n(AR, DEV - 1, asem.at[1])
    for s in range(2):
        TT[s] = AR[:, s, :].T
    tid = jnp.concatenate([TT[s, pl.ds(me, 1), :] for s in range(2)], axis=1).astype(i32) - 1
    low = (tid & 127) * 2
    group = jnp.concatenate([tid >> 7, tid >> 7], axis=1)
    LOH[...] = jnp.where(
        iota((256, 512), 0) == jnp.concatenate([low, low + 1], axis=1), 1.0, 0.0
    ).astype(bf16)
    ACC[...] = jnp.zeros((64, 512), f32)
    loads[2].wait()

    def gather_row(r, carry):
        total = ACC[...]
        for g in range(8):
            hi, lo = split(TRJ[r, :, g * 256 : (g + 1) * 256])
            y = dot(jnp.concatenate([hi, lo], axis=0), LOH[...], 1, 0)
            total = total + jnp.where(group == r * 8 + g, y[:64] + y[64:], 0.0)
        ACC[...] = total
        return carry

    lax.fori_loop(0, 4, gather_row, 0)
    for s in range(2):
        x = jnp.concatenate(
            [ACC[:, s * 128 : (s + 1) * 128], ACC[:, 256 + s * 128 : 256 + (s + 1) * 128]], axis=0
        )
        BS[:, s, :] = x.T
    BR[me] = BS[me]
    peers(lambda d, t, l: send(BS.at[d], BR.at[me], bsem, t, l).start())
    lax.fori_loop(0, 8, send_e, 0)
    send_k(KFIRST, 64)

    def place(i, carry):
        o = lax.div(i, BANDS) * 16 + lax.rem(i, BANDS) + 4 * half
        t = jnp.concatenate([TT[k, pl.ds(o, 1), :] for k in range(2)], axis=1).astype(i32) - 1
        OHR[i] = jnp.where(iota((128, 256), 0) == (t & 127), 1.0, 0.0).astype(bf16)
        return carry

    lax.fori_loop(0, 8 * BANDS, place, 0)

    S3[...] = jnp.zeros((NB, 8, 128), f32)
    swap = jnp.where(
        iota((128, 128), 1) == (iota((128, 128), 0) & 63) * 2 + (iota((128, 128), 0) >> 6), 1.0, 0.0
    ).astype(bf16)
    weight = wgt_ref[...] * vld_ref[...].astype(f32)
    loads[3].wait()
    wait_n(BR, DEV - 1, bsem.at[1])
    parts = [split(BR[:, s, :]) for s in range(2)]
    for p in range(2):
        mine = dot(M[:, :DEV], parts[0][p], 1, 0) + dot(M[:, DEV:], parts[1][p], 1, 0)
        S3[:, p, :] = dot(mine.astype(bf16), swap, 1, 0)

    def predict(b, carry):
        PR[b] = dot(S3[b].astype(bf16), JAC[b], 1, 1)
        return carry

    lax.fori_loop(0, NB, predict, 0, unroll=8)
    resid = weight * (val_ref[...] - (PR[:, 0, :] + PR[:, 1, :]))
    for p, part in enumerate(split(resid)):
        S3[:, p, :] = part.astype(f32)

    def adjoin(b, carry):
        PR[b] = dot(S3[b].astype(bf16), JAC[b], 1, 0)
        return carry

    lax.fori_loop(0, NB, adjoin, 0, unroll=8)
    placed = jnp.zeros((128, 256), f32)
    for part in split(PR[:, 0, :] + PR[:, 1, :]):
        placed = placed + dot(dot(part, swap, 1, 1).astype(bf16), M, 0, 0)
    for s in range(2):
        for w in range(2):
            CS[:, s * 2 + w, :] = placed[w * 64 : (w + 1) * 64, s * 128 : (s + 1) * 128]
    CR[me] = CS[level]
    peers(lambda d, t, l: send(CS.at[lax.div(t, 2) * 16 + l], CR.at[me], csem, t, l).start())

    wait_home(KR, 64, ksem.at[1])
    wait_home(EN, 8, esem.at[1])
    halo_k = send(KR.at[pl.ds(32, 32)], KR.at[pl.ds(64 * half, 32)], fsem.at[0], mate, lat)
    halo_e = send(EN.at[pl.ds(4, 4)], EN.at[pl.ds(8 * half, 4)], fsem.at[1], mate, lat)
    halo_k.start()
    halo_e.start()
    halo_e.wait()
    for lb in range(BANDS):
        W[lb * 4 : lb * 4 + 4] = EN[lb].astype(f32).reshape(4, 16, 128)
    WT[0] = jnp.zeros((16, 128), f32)
    WT[49] = jnp.zeros((16, 128), f32)
    lane = iota((4, 8, 128), 2)
    halo_k.wait()

    def substeps(s):
        for step in range(2):
            for lb in range(BANDS):
                rows = slice(lb * 4, lb * 4 + 4)
                if step == 0:
                    k = KR[lb * 8 + s].astype(i32).astype(f32) * KSCALE + KMID
                    k = k.reshape(4, 16, 128)
                    KF[rows] = k
                else:
                    k = KF[rows]
                WT[1 + lb * 4 : 5 + lb * 4] = k * W[rows]
            for lb in range(BANDS):
                rows = slice(lb * 4, lb * 4 + 4)
                x = WT[1 + lb * 4 : 5 + lb * 4]
                even, odd = x[:, :8], x[:, 8:]
                a = pltpu.roll(odd, 1, axis=2)
                b = pltpu.roll(even, 127, axis=2)
                a = jnp.where(lane == 0, pltpu.roll(a, 1, axis=1), a)
                b = jnp.where(lane == 127, pltpu.roll(b, 7, axis=1), b)
                ends = WT[2 + lb * 4 : 6 + lb * 4] + WT[lb * 4 : lb * 4 + 4]
                w = W[rows]
                W[rows, :8] = w[:, :8] + (ends[:, :8] + (odd + a) - 4.0 * even)
                W[rows, 8:] = w[:, 8:] + (ends[:, 8:] + (even + b) - 4.0 * odd)

    def finish(s):
        for lb in range(BANDS):
            o = s * 16 + lb + 4 * half
            t = jnp.concatenate([TT[k, pl.ds(o, 1), :] for k in range(2)], axis=1).astype(i32) - 1
            mask = iota((32, 256), 0) == (t >> 7)
            terms = []
            for w in range(2):
                term = jnp.concatenate([RT[k * 2 + w, pl.ds(o, 1), :] for k in range(2)], axis=1)
                terms.append(split(term))
            lhs = jnp.concatenate(
                [jnp.where(mask, terms[w][p].astype(f32), 0.0) for p in range(2) for w in range(2)],
                axis=0,
            ).astype(bf16)
            y = dot(lhs, OHR[s * BANDS + lb], 1, 1)
            y = y[:64] + y[64:]
            rows = slice(lb * 4, lb * 4 + 4)
            for w in range(2):
                part = slice(w * 8, w * 8 + 8)
                W[rows, part] = W[rows, part] + y[w * 32 : w * 32 + 32].reshape(4, 8, 128)

        def deliver(j, carry):
            OS[s * 8 + j] = W[pl.ds(half * 16 + j * 4, 4)].reshape(CHUNK, 128).astype(bf16)
            to = half * 8 + j
            here = (s == tm) & (to == lat)

            @pl.when(here)
            def _():
                OR[level] = OS[s * 8 + j]

            @pl.when(jnp.logical_not(here))
            def _():
                send(OS.at[s * 8 + j], OR.at[level], osem, s, to).start()

            return carry

        lax.fori_loop(0, 8, deliver, 0)

    substeps(7)
    wait_n(CR, DEV - 1, csem.at[1])
    for q in range(4):
        RT[q] = CR[:, q, :].T

    def section(i, carry):
        s = 7 - i
        finish(s)
        W[...] = W[...].astype(bf16).astype(f32)
        substeps(s - 1)
        return carry

    lax.fori_loop(0, 7, section, 0)
    finish(0)

    wait_home(OR, 64, osem.at[1])

    def widen(l, carry):
        rows = pl.ds(pl.multiple_of(l * 64, 64), 64)
        k2[rows, :] = OR[l].astype(f32)
        return carry

    lax.fori_loop(0, 64, widen, 0, unroll=4)

    def store(r, carry):
        for g in range(8):
            x = jnp.concatenate(
                [k2[pl.ds(r * 16 + w * 8 + g, 64, stride=64), :] for w in range(2)], axis=1
            )
            out_ref[r, :, g * 256 : (g + 1) * 256] = dot(x.astype(bf16), apart, 1, 1)
        return carry

    lax.fori_loop(0, 4, store, 0)

    wait_n(AR, DEV - 1, asem.at[0])
    wait_n(BS, DEV - 1, bsem.at[0])
    wait_n(CR, DEV - 1, csem.at[0])
    wait_home(ES, 8, esem.at[0])
    wait_home(KS, 64, ksem.at[0])
    wait_home(OS, 64, osem.at[0])


def per_device(traj, kap, end, jac, val, wgt, vld, own, til):
    hbm = pl.BlockSpec(memory_space=pl.ANY)
    vmem = pl.BlockSpec(memory_space=pltpu.VMEM)
    dma = pltpu.SemaphoreType.DMA
    V = pltpu.VMEM
    out = pl.pallas_call(
        kernel,
        out_shape=jax.ShapeDtypeStruct((4, 64, 2048), f32),
        in_specs=[hbm] * 4 + [vmem] * 5,
        out_specs=vmem,
        scratch_shapes=[
            V((4, 64, 2048), f32), V((4, 64, 2048), f32), V((16, 256, 128), f32),
            V((4, 16, 2048), bf16), V((16, 64, 128), f32), V((NB, 128, 128), bf16),
            V((1, 2, 128), f32), V((DEV, 2, 128), f32), V((2, 128, 128), f32),
            V((256, 512), bf16), V((64, 512), f32), V((DEV, 2, 128), f32), V((DEV, 2, 128), f32),
            V((NB, 8, 128), f32), V((NB, 8, 128), f32), V((64, 4, 128), f32), V((DEV, 4, 128), f32),
            V((4, 128, 128), f32), V((8 * BANDS, 128, 256), bf16),
            V((64, CHUNK, 128), i16), V((8 * BANDS, CHUNK, 128), i16),
            V((8, CHUNK, 128), bf16), V((BANDS, CHUNK, 128), bf16),
            V((48, 16, 128), f32), V((50, 16, 128), f32), V((48, 16, 128), f32),
            V((64, CHUNK, 128), bf16), V((64, CHUNK, 128), bf16),
            dma((4,)), dma((2,)), dma((2,)), dma((2,)), dma((2,)), dma((2,)), dma((2, 2)), dma((2,)),
        ],
        compiler_params=pltpu.CompilerParams(
            has_side_effects=True, vmem_limit_bytes=56 << 20, collective_id=0
        ),
        name="adjoint_sweep",
    )(traj[0], kap[0], end, jac, val, wgt, vld, own.reshape(1, NB), til.reshape(1, NB))
    return out[None]


def solution(mesh):
    both = ("tm", "lat")
    in_specs = (
        P("tm", "lat", None, None),
        P("tm", "lat", None, None),
        P("lat", None, None),
        P(both, None, None),
        P(both, None),
        P(both, None),
        P(both, None),
        P(both, None),
        P(both),
    )
    return jax.shard_map(
        per_device, mesh=mesh, in_specs=in_specs, out_specs=P("tm", "lat", None, None),
        check_vma=False,
    )
```

time: 110 us -> 73.6 us (0.67)
  Pallas kernels: 104 us -> 69.9 us
  local copies, waits for them, and re-layouts: 5.67 us -> 3.14 us
    pallas_call x1, Pallas kernels: 104 us -> 69.9 us  [per_device(): pl.pallas_call(kernel, out_shape=jax.ShapeDtypeStruct((4, 64, 2048), f32)...]
    transpose x1 -> x0, local copies, waits for them, and re-layouts: 2.81 us -> none  [per_device(): out.reshape(16, 4, 64, 128).transpose(1, 2, 0, 3).reshape(1, 4, 64, 2048)]
    unnamed x1, local copies, waits for them, and re-layouts: 1.37 us -> 3.14 us
    reshape x1 -> x0, local copies, waits for them, and re-layouts: 1.49 us -> none  [per_device(): out.reshape(16, 4, 64, 128).transpose(1, 2, 0, 3).reshape(1, 4, 64, 2048)]
where the time goes in v1:
time: 73.6 us; the launch traced here: 73.1 us
  Pallas kernels  69.9 us (95%)
  local copies, waits for them, and re-layouts  3.14 us (4%)
    pallas_call x1, Pallas kernels, per_device(): pl.pallas_call(kernel, out_shape=jax.ShapeDtypeStruct((4, 64, 2048), f32)...  69.9 us
    unnamed x1, local copies, waits for them, and re-layouts  3.14 us

profile of v1, /device:TPU:1, one launch (start us, length us, event | category | flops | bytes accessed | tf_op | source)
XLA Modules:
  0.0 73.1 jit_solution(15599356808848485853)
XLA Ops:
  0.0 69.9 %adjoint_sweep.1 = f32[4,64,2048]{2,1,0:T(8,128)} custom-call(f32[4,64,2048]{2,1,0:T(8,128)} %bitcast.6, f32[4,64,2048]{2,1,0:T(8,128)} %bitcast.7, bf16[4,64,2048]{2,1,0:T(8,128)(2,1)} %end_ref.1, bf16[96,128,128]{2,1,0:T(8,128)(2,1)} %jac_ref.1, f32[96,128]{1,0:T(8,128)} %val_ref.1, f32[96,128]{1,0:T(8,128)} %wgt_ref.1, s32[96,128]{1,0:T(8,128)} %vld_ref.1, ...), custom_call_target="tpu_custom_call" | custom-call | tf_op jit(solution)/shard_map/adjoint_sweep/pallas_call | solution.py:381
  69.9 3.1 %copy.11 = f32[1,4,64,2048]{3,2,1,0:T(8,128)} copy(f32[1,4,64,2048]{3,2,1,0:T(8,128)} %bitcast.5) | data formatting | bytes 4194304

commit v2 on v1

--- a/solution.py
+++ b/solution.py
@@ -29,12 +29,17 @@
     return lax.broadcasted_iota(i32, shape, dim)
 
 
+def apart_matrix():
+    target = (iota((256, 256), 1) & 127) * 2 + (iota((256, 256), 1) >> 7)
+    return jnp.where(iota((256, 256), 0) == target, 1.0, 0.0).astype(bf16)
+
+
 def kernel(
     traj_ref, kap_ref, end_ref, jac_ref, val_ref, wgt_ref, vld_ref, own_ref, til_ref,
-    out_ref,
+    OR,
     TRJ, KIN, KQ, EIN, EQ, JAC,
     AS, AR, TT, LOH, ACC, BS, BR, S3, PR, CS, CR, RT, OHR,
-    KS, KR, ES, EN, W, WT, KF, OS, OR,
+    KS, KR, ES, EN, W, WT, KF, OS,
     lsem, asem, bsem, csem, ksem, esem, fsem, osem,
 ):
     tm = lax.axis_index("tm")
@@ -102,9 +107,10 @@
     AS[0, 1:2, :] = ids[:, DEV:]
     AR[me] = AS[0]
 
-    apart = jnp.where(
-        iota((256, 256), 0) == (iota((256, 256), 1) & 127) * 2 + (iota((256, 256), 1) >> 7), 1.0, 0.0
-    ).astype(bf16)
+    pl.semaphore_wait(barrier, DEV - 1)
+    peers(lambda d, t, l: send(AS.at[0], AR.at[me], asem, t, l).start())
+
+    apart = apart_matrix()
 
     loads[0].wait()
 
@@ -131,30 +137,11 @@
 
     lax.fori_loop(0, 64, kap_level, 0, unroll=2)
 
-    loads[1].wait()
-    for r in range(4):
-        for g in range(8):
-            y = dot(EIN[r, :, g * 256 : (g + 1) * 256], apart, 1, 0)
-            EQ[g, r * 16 : (r + 1) * 16, :] = y[:, :128]
-            EQ[8 + g, r * 16 : (r + 1) * 16, :] = y[:, 128:]
-    e2 = EQ.reshape(16 * 64, 128)
-
-    def end_level(l, carry):
-        for r in range(4):
-            rows = e2[pl.ds(r * 16 + half * 8 + l, 16, stride=64), :]
-            ES[l, r * 16 : (r + 1) * 16, :] = rows.astype(bf16)
-        return carry
-
-    lax.fori_loop(0, 8, end_level, 0)
     lb_me = lat - 4 * side
 
     @pl.when(home)
     def _():
         KR[lb_me * 8 + tm] = KS[level]
-        EN[lb_me] = ES[lat - 8 * half]
-
-    pl.semaphore_wait(barrier, DEV - 1)
-    peers(lambda d, t, l: send(AS.at[0], AR.at[me], asem, t, l).start())
 
     def send_k(lo, hi):
         def step(i, carry):
@@ -210,8 +197,29 @@
         BS[:, s, :] = x.T
     BR[me] = BS[me]
     peers(lambda d, t, l: send(BS.at[d], BR.at[me], bsem, t, l).start())
+    send_k(KFIRST, 64)
+
+    loads[1].wait()
+    for r in range(4):
+        for g in range(8):
+            y = dot(EIN[r, :, g * 256 : (g + 1) * 256], apart, 1, 0)
+            EQ[g, r * 16 : (r + 1) * 16, :] = y[:, :128]
+            EQ[8 + g, r * 16 : (r + 1) * 16, :] = y[:, 128:]
+    e2 = EQ.reshape(16 * 64, 128)
+
+    def end_level(l, carry):
+        for r in range(4):
+            rows = e2[pl.ds(r * 16 + half * 8 + l, 16, stride=64), :]
+            ES[l, r * 16 : (r + 1) * 16, :] = rows.astype(bf16)
+        return carry
+
+    lax.fori_loop(0, 8, end_level, 0)
+
+    @pl.when(home)
+    def _():
+        EN[lb_me] = ES[lat - 8 * half]
+
     lax.fori_loop(0, 8, send_e, 0)
-    send_k(KFIRST, 64)
 
     def place(i, carry):
         o = lax.div(i, BANDS) * 16 + lax.rem(i, BANDS) + 4 * half
@@ -315,6 +323,7 @@
                 W[rows, part] = W[rows, part] + y[w * 32 : w * 32 + 32].reshape(4, 8, 128)
 
         def deliver(j, carry):
+            j = lax.rem(j + lat + pair * 2, 8)
             OS[s * 8 + j] = W[pl.ds(half * 16 + j * 4, 4)].reshape(CHUNK, 128).astype(bf16)
             to = half * 8 + j
             here = (s == tm) & (to == lat)
@@ -347,23 +356,6 @@
     finish(0)
 
     wait_home(OR, 64, osem.at[1])
-
-    def widen(l, carry):
-        rows = pl.ds(pl.multiple_of(l * 64, 64), 64)
-        k2[rows, :] = OR[l].astype(f32)
-        return carry
-
-    lax.fori_loop(0, 64, widen, 0, unroll=4)
-
-    def store(r, carry):
-        for g in range(8):
-            x = jnp.concatenate(
-                [k2[pl.ds(r * 16 + w * 8 + g, 64, stride=64), :] for w in range(2)], axis=1
-            )
-            out_ref[r, :, g * 256 : (g + 1) * 256] = dot(x.astype(bf16), apart, 1, 1)
-        return carry
-
-    lax.fori_loop(0, 4, store, 0)
 
     wait_n(AR, DEV - 1, asem.at[0])
     wait_n(BS, DEV - 1, bsem.at[0])
@@ -371,6 +363,29 @@
     wait_home(ES, 8, esem.at[0])
     wait_home(KS, 64, ksem.at[0])
     wait_home(OS, 64, osem.at[0])
+
+
+def decode(or_ref, out_ref, wide, rows, sem):
+    apart = apart_matrix()
+
+    def widen(l, carry):
+        wide[pl.ds(pl.multiple_of(l * 64, 64), 64), :] = or_ref[l].astype(f32)
+        return carry
+
+    lax.fori_loop(0, 64, widen, 0, unroll=4)
+
+    def copy(r):
+        return pltpu.make_async_copy(rows.at[r], out_ref.at[r], sem.at[r])
+
+    for r in range(4):
+        for g in range(8):
+            x = jnp.concatenate(
+                [wide[pl.ds(r * 16 + w * 8 + g, 64, stride=64), :] for w in range(2)], axis=1
+            )
+            rows[r, :, g * 256 : (g + 1) * 256] = dot(x.astype(bf16), apart, 1, 1)
+        copy(r).start()
+    for r in range(4):
+        copy(r).wait()
 
 
 def per_device(traj, kap, end, jac, val, wgt, vld, own, til):
@@ -380,7 +395,7 @@
     V = pltpu.VMEM
     out = pl.pallas_call(
         kernel,
-        out_shape=jax.ShapeDtypeStruct((4, 64, 2048), f32),
+        out_shape=jax.ShapeDtypeStruct((64, CHUNK, 128), bf16),
         in_specs=[hbm] * 4 + [vmem] * 5,
         out_specs=vmem,
         scratch_shapes=[
@@ -393,7 +408,7 @@
             V((64, CHUNK, 128), i16), V((8 * BANDS, CHUNK, 128), i16),
             V((8, CHUNK, 128), bf16), V((BANDS, CHUNK, 128), bf16),
             V((48, 16, 128), f32), V((50, 16, 128), f32), V((48, 16, 128), f32),
-            V((64, CHUNK, 128), bf16), V((64, CHUNK, 128), bf16),
+            V((64, CHUNK, 128), bf16),
             dma((4,)), dma((2,)), dma((2,)), dma((2,)), dma((2,)), dma((2,)), dma((2, 2)), dma((2,)),
         ],
         compiler_params=pltpu.CompilerParams(
@@ -401,6 +416,14 @@
         ),
         name="adjoint_sweep",
     )(traj[0], kap[0], end, jac, val, wgt, vld, own.reshape(1, NB), til.reshape(1, NB))
+    out = pl.pallas_call(
+        decode,
+        out_shape=jax.ShapeDtypeStruct((4, 64, 2048), f32),
+        in_specs=[vmem],
+        out_specs=hbm,
+        scratch_shapes=[V((4096, 128), f32), V((4, 64, 2048), f32), dma((4,))],
+        name="adjoint_decode",
+    )(out)
     return out[None]
 
 

time: 73.6 us -> 72.9 us (level)
  local copies, waits for them, and re-layouts: 3.14 us -> 0 us
  Pallas kernels: 69.9 us -> 72.7 us
    unnamed x1 -> x0, local copies, waits for them, and re-layouts: 3.14 us -> none
    pallas_call x1 -> x2, Pallas kernels: 69.9 us -> 72.7 us  [the longest x1 69.1 us: per_device(): pl.pallas_call(kernel, out_shape=jax.ShapeDtypeStruct((64, CHUNK, 128), b...]
where the time goes in v2:
time: 72.9 us; the launch traced here: 72.7 us
  Pallas kernels  72.7 us (100%)
    pallas_call x1, Pallas kernels, per_device(): pl.pallas_call(kernel, out_shape=jax.ShapeDtypeStruct((64, CHUNK, 128), b...  69.1 us
    pallas_call x1, Pallas kernels, per_device(): pl.pallas_call(decode, out_shape=jax.ShapeDtypeStruct((4, 64, 2048), f32)...  3.64 us

profile of v2, /device:TPU:1, one launch (start us, length us, event | category | flops | bytes accessed | tf_op | source)
XLA Modules:
  0.0 72.7 jit_solution(10722769741111633320)
XLA Ops:
  0.0 69.1 %adjoint_sweep.1.or_ref = bf16[64,64,128]{2,1,0:T(8,128)(2,1)} custom-call(f32[4,64,2048]{2,1,0:T(8,128)} %bitcast.5, f32[4,64,2048]{2,1,0:T(8,128)} %bitcast.6, bf16[4,64,2048]{2,1,0:T(8,128)(2,1)} %end_ref.1, bf16[96,128,128]{2,1,0:T(8,128)(2,1)} %jac_ref.1, f32[96,128]{1,0:T(8,128)} %val_ref.1, f32[96,128]{1,0:T(8,128)} %wgt_ref.1, s32[96,128]{1,0:T(8,128)} %vld_ref.1, ...), custom_call_target="tpu_custom_call" | custom-call | tf_op jit(solution)/shard_map/adjoint_sweep/pallas_call | solution.py:396
  69.1 3.6 %adjoint_decode.1 = f32[4,64,2048]{2,1,0:T(8,128)} custom-call(bf16[64,64,128]{2,1,0:T(8,128)(2,1)} %adjoint_sweep.1.or_ref), custom_call_target="tpu_custom_call" | custom-call | tf_op jit(solution)/shard_map/adjoint_decode/pallas_call | solution.py:419

commit v3 on v2

--- a/solution.py
+++ b/solution.py
@@ -11,7 +11,7 @@
 DEV = 128
 NB = 96
 BANDS = 12
-KFIRST = 32
+KFIRST, KNEXT = 8, 8
 CHUNK = 64
 KMID, KSCALE = 0.13, 0.11 / 32700.0
 
@@ -59,7 +59,7 @@
             fn(d, lax.div(d, 16), lax.rem(d, 16))
             return carry
 
-        lax.fori_loop(1, DEV, step, 0)
+        lax.fori_loop(1, DEV, step, 0, unroll=4)
 
     def send(src, dst, sems, t, l):
         return pltpu.make_async_remote_copy(
@@ -169,6 +169,7 @@
     send_k(0, KFIRST)
 
     wait_n(AR, DEV - 1, asem.at[1])
+    send_k(KFIRST, KNEXT)
     for s in range(2):
         TT[s] = AR[:, s, :].T
     tid = jnp.concatenate([TT[s, pl.ds(me, 1), :] for s in range(2)], axis=1).astype(i32) - 1
@@ -197,7 +198,7 @@
         BS[:, s, :] = x.T
     BR[me] = BS[me]
     peers(lambda d, t, l: send(BS.at[d], BR.at[me], bsem, t, l).start())
-    send_k(KFIRST, 64)
+    send_k(KNEXT, 64)
 
     loads[1].wait()
     for r in range(4):
@@ -322,23 +323,31 @@
                 part = slice(w * 8, w * 8 + 8)
                 W[rows, part] = W[rows, part] + y[w * 32 : w * 32 + 32].reshape(4, 8, 128)
 
-        def deliver(j, carry):
-            j = lax.rem(j + lat + pair * 2, 8)
-            OS[s * 8 + j] = W[pl.ds(half * 16 + j * 4, 4)].reshape(CHUNK, 128).astype(bf16)
-            to = half * 8 + j
-            here = (s == tm) & (to == lat)
-
-            @pl.when(here)
-            def _():
-                OR[level] = OS[s * 8 + j]
-
-            @pl.when(jnp.logical_not(here))
-            def _():
-                send(OS.at[s * 8 + j], OR.at[level], osem, s, to).start()
-
+        for j in range(8):
+            rows = W[pl.ds(half * 16 + j * 4, 4)]
+            OS[s * 8 + j] = rows.reshape(CHUNK, 128).astype(bf16)
+
+    def deliver(s, j):
+        here = (s == tm) & (half * 8 + j == lat)
+
+        @pl.when(jnp.logical_not(here))
+        def _():
+            send(OS.at[s * 8 + j], OR.at[level], osem, s, half * 8 + j).start()
+
+    def deliver_early(s):
+        def step(i, carry):
+            deliver(s, lax.rem(i + lat + pair * 2, 8))
             return carry
 
-        lax.fori_loop(0, 8, deliver, 0)
+        lax.fori_loop(0, 8, step, 0)
+
+    def deliver_late(i, carry):
+        q = lax.rem(i, 5)
+        s = jnp.int32(0)
+        for k, v in enumerate([0, 2, 4, 6, 1]):
+            s = jnp.where(q == k, v, s)
+        deliver(s, lax.rem(lax.div(i, 5) + lat + pair * 2 + q, 8))
+        return carry
 
     substeps(7)
     wait_n(CR, DEV - 1, csem.at[1])
@@ -348,12 +357,22 @@
     def section(i, carry):
         s = 7 - i
         finish(s)
+
+        @pl.when((s == 7) | (s == 5) | (s == 3))
+        def _():
+            deliver_early(s)
+
         W[...] = W[...].astype(bf16).astype(f32)
         substeps(s - 1)
         return carry
 
     lax.fori_loop(0, 7, section, 0)
     finish(0)
+    lax.fori_loop(0, 40, deliver_late, 0)
+
+    @pl.when(home)
+    def _():
+        OR[level] = OS[tm * 8 + lat - half * 8]
 
     wait_home(OR, 64, osem.at[1])
 

time: 72.9 us -> 66.7 us (0.915)
  Pallas kernels: 72.7 us -> 66.5 us
    pallas_call x1, Pallas kernels: 69.1 us -> 62.9 us  [per_device(): pl.pallas_call(kernel, out_shape=jax.ShapeDtypeStruct((64, CHUNK, 128), b...]
where the time goes in v3:
time: 66.7 us; the launch traced here: 66.5 us
  Pallas kernels  66.5 us (100%)
    pallas_call x1, Pallas kernels, per_device(): pl.pallas_call(kernel, out_shape=jax.ShapeDtypeStruct((64, CHUNK, 128), b...  62.9 us
    pallas_call x1, Pallas kernels, per_device(): pl.pallas_call(decode, out_shape=jax.ShapeDtypeStruct((4, 64, 2048), f32)...  3.64 us

profile of v3, /device:TPU:1, one launch (start us, length us, event | category | flops | bytes accessed | tf_op | source)
XLA Modules:
  0.0 66.5 jit_solution(15112222964682611168)
XLA Ops:
  0.0 62.9 %adjoint_sweep.1.or_ref = bf16[64,64,128]{2,1,0:T(8,128)(2,1)} custom-call(f32[4,64,2048]{2,1,0:T(8,128)} %bitcast.5, f32[4,64,2048]{2,1,0:T(8,128)} %bitcast.6, bf16[4,64,2048]{2,1,0:T(8,128)(2,1)} %end_ref.1, bf16[96,128,128]{2,1,0:T(8,128)(2,1)} %jac_ref.1, f32[96,128]{1,0:T(8,128)} %val_ref.1, f32[96,128]{1,0:T(8,128)} %wgt_ref.1, s32[96,128]{1,0:T(8,128)} %vld_ref.1, ...), custom_call_target="tpu_custom_call" | custom-call | tf_op jit(solution)/shard_map/adjoint_sweep/pallas_call | solution.py:415
  62.9 3.6 %adjoint_decode.1 = f32[4,64,2048]{2,1,0:T(8,128)} custom-call(bf16[64,64,128]{2,1,0:T(8,128)(2,1)} %adjoint_sweep.1.or_ref), custom_call_target="tpu_custom_call" | custom-call | tf_op jit(solution)/shard_map/adjoint_decode/pallas_call | solution.py:438

commit v4 on v3

--- a/solution.py
+++ b/solution.py
@@ -11,7 +11,7 @@
 DEV = 128
 NB = 96
 BANDS = 12
-KFIRST, KNEXT = 8, 8
+KFIRST = 8
 CHUNK = 64
 KMID, KSCALE = 0.13, 0.11 / 32700.0
 
@@ -158,6 +158,7 @@
         lax.fori_loop(lo, hi, step, 0)
 
     def send_e(i, carry):
+        i = lax.rem(i + lat, 8)
         l = half * 8 + i
 
         @pl.when((l != lat) | away)
@@ -168,8 +169,30 @@
 
     send_k(0, KFIRST)
 
+    loads[1].wait()
+    for r in range(4):
+        for g in range(8):
+            y = dot(EIN[r, :, g * 256 : (g + 1) * 256], apart, 1, 0)
+            EQ[g, r * 16 : (r + 1) * 16, :] = y[:, :128]
+            EQ[8 + g, r * 16 : (r + 1) * 16, :] = y[:, 128:]
+    e2 = EQ.reshape(16 * 64, 128)
+
+    def end_level(l, carry):
+        for r in range(4):
+            rows = e2[pl.ds(r * 16 + half * 8 + l, 16, stride=64), :]
+            ES[l, r * 16 : (r + 1) * 16, :] = rows.astype(bf16)
+        return carry
+
+    lax.fori_loop(0, 8, end_level, 0)
+
+    @pl.when(home)
+    def _():
+        EN[lb_me] = ES[lat - 8 * half]
+
+    lax.fori_loop(0, 8, send_e, 0)
+    S3[...] = jnp.zeros((NB, 8, 128), f32)
+
     wait_n(AR, DEV - 1, asem.at[1])
-    send_k(KFIRST, KNEXT)
     for s in range(2):
         TT[s] = AR[:, s, :].T
     tid = jnp.concatenate([TT[s, pl.ds(me, 1), :] for s in range(2)], axis=1).astype(i32) - 1
@@ -198,29 +221,8 @@
         BS[:, s, :] = x.T
     BR[me] = BS[me]
     peers(lambda d, t, l: send(BS.at[d], BR.at[me], bsem, t, l).start())
-    send_k(KNEXT, 64)
-
-    loads[1].wait()
-    for r in range(4):
-        for g in range(8):
-            y = dot(EIN[r, :, g * 256 : (g + 1) * 256], apart, 1, 0)
-            EQ[g, r * 16 : (r + 1) * 16, :] = y[:, :128]
-            EQ[8 + g, r * 16 : (r + 1) * 16, :] = y[:, 128:]
-    e2 = EQ.reshape(16 * 64, 128)
-
-    def end_level(l, carry):
-        for r in range(4):
-            rows = e2[pl.ds(r * 16 + half * 8 + l, 16, stride=64), :]
-            ES[l, r * 16 : (r + 1) * 16, :] = rows.astype(bf16)
-        return carry
-
-    lax.fori_loop(0, 8, end_level, 0)
-
-    @pl.when(home)
-    def _():
-        EN[lb_me] = ES[lat - 8 * half]
-
-    lax.fori_loop(0, 8, send_e, 0)
+    send_k(KFIRST, 64)
+
 
     def place(i, carry):
         o = lax.div(i, BANDS) * 16 + lax.rem(i, BANDS) + 4 * half
@@ -230,7 +232,6 @@
 
     lax.fori_loop(0, 8 * BANDS, place, 0)
 
-    S3[...] = jnp.zeros((NB, 8, 128), f32)
     swap = jnp.where(
         iota((128, 128), 1) == (iota((128, 128), 0) & 63) * 2 + (iota((128, 128), 0) >> 6), 1.0, 0.0
     ).astype(bf16)
@@ -246,7 +247,7 @@
         PR[b] = dot(S3[b].astype(bf16), JAC[b], 1, 1)
         return carry
 
-    lax.fori_loop(0, NB, predict, 0, unroll=8)
+    lax.fori_loop(0, NB, predict, 0, unroll=32)
     resid = weight * (val_ref[...] - (PR[:, 0, :] + PR[:, 1, :]))
     for p, part in enumerate(split(resid)):
         S3[:, p, :] = part.astype(f32)
@@ -255,7 +256,7 @@
         PR[b] = dot(S3[b].astype(bf16), JAC[b], 1, 0)
         return carry
 
-    lax.fori_loop(0, NB, adjoin, 0, unroll=8)
+    lax.fori_loop(0, NB, adjoin, 0, unroll=32)
     placed = jnp.zeros((128, 256), f32)
     for part in split(PR[:, 0, :] + PR[:, 1, :]):
         placed = placed + dot(dot(part, swap, 1, 1).astype(bf16), M, 0, 0)

time: 66.7 us -> 65 us (0.975)
  Pallas kernels: 66.5 us -> 64.8 us
    pallas_call x1, Pallas kernels: 62.9 us -> 61.1 us  [per_device(): pl.pallas_call(kernel, out_shape=jax.ShapeDtypeStruct((64, CHUNK, 128), b...]
where the time goes in v4:
time: 65 us; the launch traced here: 64.8 us
  Pallas kernels  64.8 us (100%)
    pallas_call x1, Pallas kernels, per_device(): pl.pallas_call(kernel, out_shape=jax.ShapeDtypeStruct((64, CHUNK, 128), b...  61.1 us
    pallas_call x1, Pallas kernels, per_device(): pl.pallas_call(decode, out_shape=jax.ShapeDtypeStruct((4, 64, 2048), f32)...  3.64 us

profile of v4, /device:TPU:1, one launch (start us, length us, event | category | flops | bytes accessed | tf_op | source)
XLA Modules:
  0.0 64.8 jit_solution(5667745037710668558)
XLA Ops:
  0.0 61.1 %adjoint_sweep.1.or_ref = bf16[64,64,128]{2,1,0:T(8,128)(2,1)} custom-call(f32[4,64,2048]{2,1,0:T(8,128)} %bitcast.5, f32[4,64,2048]{2,1,0:T(8,128)} %bitcast.6, bf16[4,64,2048]{2,1,0:T(8,128)(2,1)} %end_ref.1, bf16[96,128,128]{2,1,0:T(8,128)(2,1)} %jac_ref.1, f32[96,128]{1,0:T(8,128)} %val_ref.1, f32[96,128]{1,0:T(8,128)} %wgt_ref.1, s32[96,128]{1,0:T(8,128)} %vld_ref.1, ...), custom_call_target="tpu_custom_call" | custom-call | tf_op jit(solution)/shard_map/adjoint_sweep/pallas_call | solution.py:416
  61.1 3.6 %adjoint_decode.1 = f32[4,64,2048]{2,1,0:T(8,128)} custom-call(bf16[64,64,128]{2,1,0:T(8,128)(2,1)} %adjoint_sweep.1.or_ref), custom_call_target="tpu_custom_call" | custom-call | tf_op jit(solution)/shard_map/adjoint_decode/pallas_call | solution.py:439

commit v5 on v4

--- a/solution.py
+++ b/solution.py
@@ -39,7 +39,7 @@
     OR,
     TRJ, KIN, KQ, EIN, EQ, JAC,
     AS, AR, TT, LOH, ACC, BS, BR, S3, PR, CS, CR, RT, OHR,
-    KS, KR, ES, EN, W, WT, KF, OS,
+    KS, KR, ES, EN, W, WT, KF, FB, OS,
     lsem, asem, bsem, csem, ksem, esem, fsem, osem,
 ):
     tm = lax.axis_index("tm")
@@ -304,7 +304,7 @@
                 W[rows, :8] = w[:, :8] + (ends[:, :8] + (odd + a) - 4.0 * even)
                 W[rows, 8:] = w[:, 8:] + (ends[:, 8:] + (even + b) - 4.0 * odd)
 
-    def finish(s):
+    def force(s):
         for lb in range(BANDS):
             o = s * 16 + lb + 4 * half
             t = jnp.concatenate([TT[k, pl.ds(o, 1), :] for k in range(2)], axis=1).astype(i32) - 1
@@ -322,7 +322,12 @@
             rows = slice(lb * 4, lb * 4 + 4)
             for w in range(2):
                 part = slice(w * 8, w * 8 + 8)
-                W[rows, part] = W[rows, part] + y[w * 32 : w * 32 + 32].reshape(4, 8, 128)
+                FB[rows, part] = y[w * 32 : w * 32 + 32].reshape(4, 8, 128)
+
+    def finish(s):
+        for lb in range(BANDS):
+            rows = slice(lb * 4, lb * 4 + 4)
+            W[rows] = W[rows] + FB[rows]
 
         for j in range(8):
             rows = W[pl.ds(half * 16 + j * 4, 4)]
@@ -354,6 +359,7 @@
     wait_n(CR, DEV - 1, csem.at[1])
     for q in range(4):
         RT[q] = CR[:, q, :].T
+    force(7)
 
     def section(i, carry):
         s = 7 - i
@@ -364,6 +370,7 @@
             deliver_early(s)
 
         W[...] = W[...].astype(bf16).astype(f32)
+        force(s - 1)
         substeps(s - 1)
         return carry
 
@@ -427,7 +434,7 @@
             V((4, 128, 128), f32), V((8 * BANDS, 128, 256), bf16),
             V((64, CHUNK, 128), i16), V((8 * BANDS, CHUNK, 128), i16),
             V((8, CHUNK, 128), bf16), V((BANDS, CHUNK, 128), bf16),
-            V((48, 16, 128), f32), V((50, 16, 128), f32), V((48, 16, 128), f32),
+            V((48, 16, 128), f32), V((50, 16, 128), f32), V((48, 16, 128), f32), V((48, 16, 128), f32),
             V((64, CHUNK, 128), bf16),
             dma((4,)), dma((2,)), dma((2,)), dma((2,)), dma((2,)), dma((2,)), dma((2, 2)), dma((2,)),
         ],

time: 65 us -> 64.5 us (level)
  no operation moved by 1% of the time
where the time goes in v5:
time: 64.5 us; the launch traced here: 64.3 us
  Pallas kernels  64.3 us (100%)
    pallas_call x1, Pallas kernels, per_device(): pl.pallas_call(kernel, out_shape=jax.ShapeDtypeStruct((64, CHUNK, 128), b...  60.6 us
    pallas_call x1, Pallas kernels, per_device(): pl.pallas_call(decode, out_shape=jax.ShapeDtypeStruct((4, 64, 2048), f32)...  3.64 us

profile of v5, /device:TPU:1, one launch (start us, length us, event | category | flops | bytes accessed | tf_op | source)
XLA Modules:
  0.0 64.3 jit_solution(2185847656174500854)
XLA Ops:
  0.0 60.6 %adjoint_sweep.1.or_ref = bf16[64,64,128]{2,1,0:T(8,128)(2,1)} custom-call(f32[4,64,2048]{2,1,0:T(8,128)} %bitcast.5, f32[4,64,2048]{2,1,0:T(8,128)} %bitcast.6, bf16[4,64,2048]{2,1,0:T(8,128)(2,1)} %end_ref.1, bf16[96,128,128]{2,1,0:T(8,128)(2,1)} %jac_ref.1, f32[96,128]{1,0:T(8,128)} %val_ref.1, f32[96,128]{1,0:T(8,128)} %wgt_ref.1, s32[96,128]{1,0:T(8,128)} %vld_ref.1, ...), custom_call_target="tpu_custom_call" | custom-call | tf_op jit(solution)/shard_map/adjoint_sweep/pallas_call | solution.py:423
  60.6 3.6 %adjoint_decode.1 = f32[4,64,2048]{2,1,0:T(8,128)} custom-call(bf16[64,64,128]{2,1,0:T(8,128)(2,1)} %adjoint_sweep.1.or_ref), custom_call_target="tpu_custom_call" | custom-call | tf_op jit(solution)/shard_map/adjoint_decode/pallas_call | solution.py:446

commit v6 on v5

--- a/solution.py
+++ b/solution.py
@@ -38,7 +38,7 @@
     traj_ref, kap_ref, end_ref, jac_ref, val_ref, wgt_ref, vld_ref, own_ref, til_ref,
     OR,
     TRJ, KIN, KQ, EIN, EQ, JAC,
-    AS, AR, TT, LOH, ACC, BS, BR, S3, PR, CS, CR, RT, OHR,
+    AS, AR, TT, LOH, ACC, BS, BR, MX, S3, S4, PR, CS, CR, RT, OHR,
     KS, KR, ES, EN, W, WT, KF, FB, OS,
     lsem, asem, bsem, csem, ksem, esem, fsem, osem,
 ):
@@ -190,7 +190,8 @@
         EN[lb_me] = ES[lat - 8 * half]
 
     lax.fori_loop(0, 8, send_e, 0)
-    S3[...] = jnp.zeros((NB, 8, 128), f32)
+    S3[...] = jnp.zeros((NB // 2, 8, 128), f32)
+    S4[...] = jnp.zeros((NB // 2, 8, 256), f32)
 
     wait_n(AR, DEV - 1, asem.at[1])
     for s in range(2):
@@ -235,30 +236,38 @@
     swap = jnp.where(
         iota((128, 128), 1) == (iota((128, 128), 0) & 63) * 2 + (iota((128, 128), 0) >> 6), 1.0, 0.0
     ).astype(bf16)
-    weight = wgt_ref[...] * vld_ref[...].astype(f32)
     loads[3].wait()
     wait_n(BR, DEV - 1, bsem.at[1])
     parts = [split(BR[:, s, :]) for s in range(2)]
     for p in range(2):
         mine = dot(M[:, :DEV], parts[0][p], 1, 0) + dot(M[:, DEV:], parts[1][p], 1, 0)
-        S3[:, p, :] = dot(mine.astype(bf16), swap, 1, 0)
-
-    def predict(b, carry):
-        PR[b] = dot(S3[b].astype(bf16), JAC[b], 1, 1)
-        return carry
-
-    lax.fori_loop(0, NB, predict, 0, unroll=32)
-    resid = weight * (val_ref[...] - (PR[:, 0, :] + PR[:, 1, :]))
-    for p, part in enumerate(split(resid)):
-        S3[:, p, :] = part.astype(f32)
-
-    def adjoin(b, carry):
-        PR[b] = dot(S3[b].astype(bf16), JAC[b], 1, 0)
-        return carry
-
-    lax.fori_loop(0, NB, adjoin, 0, unroll=32)
+        MX[p] = dot(mine.astype(bf16), swap, 1, 0)
+    pairs = JAC.reshape(NB // 2, 256, 128)
+    for q in range(2):
+        for p in range(2):
+            S3[:, q * 2 + p, :] = MX[p, pl.ds(q, NB // 2, stride=2), :]
+
+    def predict(k, carry):
+        PR[k] = dot(S3[k].astype(bf16), pairs[k], 1, 1)
+        return carry
+
+    lax.fori_loop(0, NB // 2, predict, 0, unroll=16)
+    for q in range(2):
+        rows, cols = pl.ds(q, NB // 2, stride=2), slice(q * 128, q * 128 + 128)
+        weight = wgt_ref[rows, :] * vld_ref[rows, :].astype(f32)
+        pred = PR[:, q * 2, cols] + PR[:, q * 2 + 1, cols]
+        for p, part in enumerate(split(weight * (val_ref[rows, :] - pred))):
+            S4[:, q * 2 + p, cols] = part.astype(f32)
+
+    def adjoin(k, carry):
+        S3[k] = dot(S4[k].astype(bf16), pairs[k], 1, 0)
+        return carry
+
+    lax.fori_loop(0, NB // 2, adjoin, 0, unroll=16)
+    for q in range(2):
+        MX[0, pl.ds(q, NB // 2, stride=2), :] = S3[:, q * 2, :] + S3[:, q * 2 + 1, :]
     placed = jnp.zeros((128, 256), f32)
-    for part in split(PR[:, 0, :] + PR[:, 1, :]):
+    for part in split(MX[0]):
         placed = placed + dot(dot(part, swap, 1, 1).astype(bf16), M, 0, 0)
     for s in range(2):
         for w in range(2):
@@ -376,7 +385,7 @@
 
     lax.fori_loop(0, 7, section, 0)
     finish(0)
-    lax.fori_loop(0, 40, deliver_late, 0)
+    lax.fori_loop(0, 40, deliver_late, 0, unroll=4)
 
     @pl.when(home)
     def _():
@@ -392,22 +401,24 @@
     wait_home(OS, 64, osem.at[0])
 
 
-def decode(or_ref, out_ref, wide, rows, sem):
+def decode(or_ref, out_ref, chunks, wide, rows, isem, osem):
+    def load(r):
+        return pltpu.make_async_copy(
+            or_ref.at[:, pl.ds(r * 16, 16), :], chunks.at[r], isem.at[r]
+        )
+
+    def copy(r):
+        return pltpu.make_async_copy(rows.at[r], out_ref.at[r], osem.at[r])
+
+    for r in range(4):
+        load(r).start()
     apart = apart_matrix()
-
-    def widen(l, carry):
-        wide[pl.ds(pl.multiple_of(l * 64, 64), 64), :] = or_ref[l].astype(f32)
-        return carry
-
-    lax.fori_loop(0, 64, widen, 0, unroll=4)
-
-    def copy(r):
-        return pltpu.make_async_copy(rows.at[r], out_ref.at[r], sem.at[r])
-
     for r in range(4):
+        load(r).wait()
+        wide[r] = chunks[r].astype(f32).reshape(1024, 128)
         for g in range(8):
             x = jnp.concatenate(
-                [wide[pl.ds(r * 16 + w * 8 + g, 64, stride=64), :] for w in range(2)], axis=1
+                [wide[r, pl.ds(w * 8 + g, 64, stride=16), :] for w in range(2)], axis=1
             )
             rows[r, :, g * 256 : (g + 1) * 256] = dot(x.astype(bf16), apart, 1, 1)
         copy(r).start()
@@ -430,7 +441,8 @@
             V((4, 16, 2048), bf16), V((16, 64, 128), f32), V((NB, 128, 128), bf16),
             V((1, 2, 128), f32), V((DEV, 2, 128), f32), V((2, 128, 128), f32),
             V((256, 512), bf16), V((64, 512), f32), V((DEV, 2, 128), f32), V((DEV, 2, 128), f32),
-            V((NB, 8, 128), f32), V((NB, 8, 128), f32), V((64, 4, 128), f32), V((DEV, 4, 128), f32),
+            V((2, NB, 128), f32), V((NB // 2, 8, 128), f32), V((NB // 2, 8, 256), f32),
+            V((NB // 2, 8, 256), f32), V((64, 4, 128), f32), V((DEV, 4, 128), f32),
             V((4, 128, 128), f32), V((8 * BANDS, 128, 256), bf16),
             V((64, CHUNK, 128), i16), V((8 * BANDS, CHUNK, 128), i16),
             V((8, CHUNK, 128), bf16), V((BANDS, CHUNK, 128), bf16),
@@ -446,9 +458,12 @@
     out = pl.pallas_call(
         decode,
         out_shape=jax.ShapeDtypeStruct((4, 64, 2048), f32),
-        in_specs=[vmem],
+        in_specs=[hbm],
         out_specs=hbm,
-        scratch_shapes=[V((4096, 128), f32), V((4, 64, 2048), f32), dma((4,))],
+        scratch_shapes=[
+            V((4, 64, 16, 128), bf16), V((4, 1024, 128), f32), V((4, 64, 2048), f32),
+            dma((4,)), dma((4,)),
+        ],
         name="adjoint_decode",
     )(out)
     return out[None]

time: 64.5 us -> 64.2 us (level)
  no operation moved by 1% of the time
where the time goes in v6:
time: 64.2 us; the launch traced here: 64 us
  Pallas kernels  64 us (100%)
    pallas_call x1, Pallas kernels, per_device(): pl.pallas_call(kernel, out_shape=jax.ShapeDtypeStruct((64, CHUNK, 128), b...  60.4 us
    pallas_call x1, Pallas kernels, per_device(): pl.pallas_call(decode, out_shape=jax.ShapeDtypeStruct((4, 64, 2048), f32)...  3.59 us

profile of v6, /device:TPU:1, one launch (start us, length us, event | category | flops | bytes accessed | tf_op | source)
XLA Modules:
  0.0 64.0 jit_solution(7122288558017235155)
XLA Ops:
  0.0 60.4 %adjoint_sweep.1.or_ref = bf16[64,64,128]{2,1,0:T(8,128)(2,1)} custom-call(f32[4,64,2048]{2,1,0:T(8,128)} %bitcast.5, f32[4,64,2048]{2,1,0:T(8,128)} %bitcast.6, bf16[4,64,2048]{2,1,0:T(8,128)(2,1)} %end_ref.1, bf16[96,128,128]{2,1,0:T(8,128)(2,1)} %jac_ref.1, f32[96,128]{1,0:T(8,128)} %val_ref.1, f32[96,128]{1,0:T(8,128)} %wgt_ref.1, s32[96,128]{1,0:T(8,128)} %vld_ref.1, ...), custom_call_target="tpu_custom_call" | custom-call | tf_op jit(solution)/shard_map/adjoint_sweep/pallas_call | solution.py:434
  60.4 3.6 %adjoint_decode.1 = f32[4,64,2048]{2,1,0:T(8,128)} custom-call(bf16[64,64,128]{2,1,0:T(8,128)(2,1)} %adjoint_sweep.1.or_ref), custom_call_target="tpu_custom_call" | custom-call | tf_op jit(solution)/shard_map/adjoint_decode/pallas_call | solution.py:458
